TPU v7x, 256 devices: a whole 4x4x8 slice. The times are simulated.
256 devices in a mesh: dp: 16 (over z, core), seq: 4 (over x), section: 4 (over y).
Axes of the slice: x: 4, y: 4, z: 8, core: 2. Of those that a mesh axis runs over, the one named last changes fastest.
Arguments:
- projected: bfloat16 [4, 4, 96, 128, 4096], P('section', 'seq', 'dp'), may hold values from -6 to 6
- dest_owner: int32 [4, 4, 96], P('section', 'seq', 'dp'), may hold values from 0 to 15, as said below
- slot_from: int32 [4, 16, 24], P('section', 'dp', 'seq'), may hold values from 0 to 15, as said below
- doc_starts: int32 [4, 16, 24], P('section', 'dp', 'seq'), may hold values from 0 to 1, as said below
- live_rows: int32 [4, 16, 24], P('section', 'dp', 'seq'), may hold values from 1 to 128, as said below
Outputs:
- attended: bfloat16 [4, 16, 3072, 2048], P('section', 'dp', 'seq')
Inputs may be any that keep to these rules, and one draw needn't show every extreme that they name: `dest_owner`: in each column (t, s), every source device sends at most 1 block to one owner, some source sends exactly 1 block to some owner, and every owner receives exactly 6 blocks. Over all 4 columns (t, s) of one section t, source a sends at most 2 blocks to one owner, and some source sends exactly 2 to some owner. For owner o in column (t, s), slot_from[t, o, s * 6 + j] over j names each of the 6 numbers of the blocks that went to o in that column once. `doc_starts`: the first block of every pack begins a document; a document spans at most 8 blocks, and in every pack some document spans exactly 8. `live_rows`: 128 in every block but the last block of a document (the block before the next start, or the pack's last block).
All inputs are finite; a program needn't handle non-finite values.
Results may differ from a plain program's by a relative error of at most 0.0069.
Values may be sent and summed in bfloat16 or wider, within the bound.
No kernel may reach another device: no remote copies, remote signals or barrier semaphores. Data moves between devices by JAX's collectives and lax.ppermute only.
A program may use at most 128 MiB of HBM per device.

v0:
```python
import jax
import jax.numpy as jnp
from jax import lax
from jax.sharding import PartitionSpec as P

HEADS = 8
KV_HEADS = 4
HEAD_DIM = 256


score_cap = 50.0
rope_base = 10000.0


def passed_along(block, axis, distance):
    devices = range(lax.axis_size(axis))
    route = [((i - distance) % len(devices), i) for i in devices]
    return lax.ppermute(block, axis, route)


def rotate(columns, position, head_count):
    row_count = columns.shape[0]
    head_width = columns.shape[1] // head_count
    half_width = head_width // 2
    frequency = rope_base ** (-2.0 * jnp.arange(half_width, dtype=jnp.float32) / head_width)
    angles = position[:, None] * frequency[None, :]
    cosine = jnp.cos(angles)[:, None, :]
    sine_part = jnp.sin(angles)[:, None, :]
    split_heads = columns.astype(jnp.float32).reshape(row_count, head_count, head_width)
    first_half = split_heads[:, :, :half_width]
    second_half = split_heads[:, :, half_width:]
    turned = jnp.concatenate(
        [
            first_half * cosine - second_half * sine_part,
            second_half * cosine + first_half * sine_part,
        ],
        axis=2,
    )
    return turned.reshape(row_count, head_count * head_width).astype(jnp.bfloat16)


def cut_rows(array, begin_row, size):
    return lax.dynamic_slice_in_dim(array, begin_row, size, 0)


def row_tables(start_flags, live_count, prior_count, prior_first, block_rows):
    block_ids = jnp.arange(start_flags.shape[0], dtype=jnp.int32)
    doc_number = prior_count + jnp.cumsum(start_flags) - 1
    doc_first = jnp.maximum(
        prior_first, lax.cummax(jnp.where(start_flags == 1, block_ids, -1), axis=0)
    )
    row_offset = jnp.arange(block_rows, dtype=jnp.int32)
    position = (
        ((block_ids - doc_first)[:, None] * block_rows + row_offset[None, :])
        .reshape(-1)
        .astype(jnp.float32)
    )
    alive_rows = (row_offset[None, :] < live_count[:, None]).reshape(-1)
    doc_rows = jnp.repeat(doc_number, block_rows)
    query_tag = jnp.where(alive_rows, doc_rows, -2).astype(jnp.float32)
    key_tag = jnp.where(alive_rows, doc_rows, -1).astype(jnp.bfloat16)
    return (position, alive_rows, query_tag, key_tag)


def initial_state(row_count, head_count, kv_heads, head_width):
    group_size = head_count // kv_heads
    return (
        jnp.zeros((row_count, kv_heads, group_size, head_width), jnp.float32),
        jnp.zeros((row_count, kv_heads, group_size), jnp.float32),
    )


def attend(
    running,
    queries,
    query_tag,
    query_row,
    key_rows,
    values,
    key_tag,
    key_anchor,
    head_count,
    kv_heads,
):
    row_count = queries.shape[0]
    key_count = key_rows.shape[0]
    head_width = queries.shape[1] // head_count
    group_size = head_count // kv_heads
    key_index = key_anchor + jnp.arange(key_count, dtype=jnp.int32)
    allowed = (query_tag[:, None] == key_tag.astype(jnp.float32)[None, :]) & (
        key_index[None, :] <= query_row[:, None]
    )

    def compute(state):
        numerator, denominator = state
        grouped = queries.reshape(row_count, kv_heads, group_size, head_width)
        scores = jnp.einsum(
            "rhgd,khd->rhgk",
            grouped,
            key_rows.reshape(key_count, kv_heads, head_width),
            preferred_element_type=jnp.float32,
        ) * head_width ** (-0.5)
        capped = score_cap * jnp.tanh(scores / score_cap)
        weight = jnp.where(allowed[:, None, None, :], jnp.exp(capped), 0.0)
        denominator = denominator + jnp.sum(weight, axis=3)
        numerator = numerator + jnp.einsum(
            "rhgk,khd->rhgd",
            weight.astype(jnp.bfloat16),
            values.reshape(key_count, kv_heads, head_width),
            preferred_element_type=jnp.float32,
        )
        return (numerator, denominator)

    def keep(state):
        return state

    return lax.cond(jnp.any(allowed), compute, keep, running)


def attend_keys(
    running,
    queries,
    query_tag,
    query_row,
    key_rows,
    values,
    key_tag,
    key_anchor,
    head_count,
    kv_heads,
    key_step,
):

    def key_turn(state, number):
        begin_row = number * key_step
        state = attend(
            state,
            queries,
            query_tag,
            query_row,
            cut_rows(key_rows, begin_row, key_step),
            cut_rows(values, begin_row, key_step),
            cut_rows(key_tag, begin_row, key_step),
            key_anchor + begin_row,
            head_count,
            kv_heads,
        )
        return (state, None)

    running, unused = lax.scan(
        key_turn, running, jnp.arange(key_rows.shape[0] // key_step, dtype=jnp.int32)
    )
    return running


def finish(running, alive_rows, row_count, head_count, head_width):
    numerator, denominator = running
    safe_total = jnp.where(alive_rows[:, None, None], denominator, 1.0)
    averaged = jnp.where(
        alive_rows[:, None, None, None], numerator / safe_total[:, :, :, None], 0.0
    )
    return averaged.reshape(row_count, head_count * head_width).astype(jnp.bfloat16)


def send_plan(owner_list, shard_of, local_index, capacity, shard_count, dp_count):
    same_owner = (
        (owner_list[:, None] == owner_list[None, :])
        & (shard_of[:, None] == shard_of[None, :])
        & (local_index[None, :] < local_index[:, None])
    )
    ranking = jnp.sum(same_owner, axis=1)
    target = owner_list * (shard_count * capacity) + ranking
    matches = (
        target[None, :] == jnp.arange(dp_count * shard_count * capacity, dtype=jnp.int32)[:, None]
    )
    chosen = jnp.sum(
        jnp.where(matches, jnp.arange(owner_list.shape[0], dtype=jnp.int32)[None, :], 0), axis=1
    )
    return (chosen, jnp.any(matches, axis=1))


def shards(projected, dest_owner, slot_from, doc_starts, live_rows):
    sources = projected[0, 0]
    source_blocks, block_rows, full_width = sources.shape
    dp_count = lax.axis_size("dp")
    seq_count = lax.axis_size("seq")
    capacity = (source_blocks + dp_count - 1) // dp_count
    query_width = HEADS * HEAD_DIM
    key_width = KV_HEADS * HEAD_DIM
    row_count = source_blocks * block_rows
    key_step = 2 * block_rows
    owners = dest_owner[0, 0]
    slot_list = slot_from[0, 0]
    start_flags = doc_starts[0, 0]
    live_count = live_rows[0, 0]
    query_heads = HEADS // seq_count
    key_heads = KV_HEADS // seq_count
    total_rows = seq_count * row_count
    total_blocks = seq_count * source_blocks
    pooled = (total_blocks + dp_count - 1) // dp_count
    query_step = 4 * block_rows
    all_owners, all_slots, all_starts, all_live = (
        lax.all_gather(owners, "seq", axis=0, tiled=True),
        lax.all_gather(slot_list, "seq", axis=0, tiled=True),
        lax.all_gather(start_flags, "seq", axis=0, tiled=True),
        lax.all_gather(live_count, "seq", axis=0, tiled=True),
    )
    query_part = sources[:, :, :query_width].reshape(
        source_blocks, block_rows, seq_count, query_heads * HEAD_DIM
    )
    key_part = sources[:, :, query_width : query_width + key_width].reshape(
        source_blocks, block_rows, seq_count, key_heads * HEAD_DIM
    )
    value_part = sources[:, :, query_width + key_width :].reshape(
        source_blocks, block_rows, seq_count, key_heads * HEAD_DIM
    )
    grouped_in = (
        lax.all_to_all(query_part, "seq", split_axis=2, concat_axis=0, tiled=True),
        lax.all_to_all(key_part, "seq", split_axis=2, concat_axis=0, tiled=True),
        lax.all_to_all(value_part, "seq", split_axis=2, concat_axis=0, tiled=True),
    )
    shard_of = jnp.repeat(jnp.arange(seq_count, dtype=jnp.int32), source_blocks)
    chosen, filled = send_plan(
        all_owners,
        jnp.zeros_like(all_owners),
        jnp.arange(total_blocks, dtype=jnp.int32),
        pooled,
        1,
        dp_count,
    )

    def outgoing_of(columns):
        picked = jnp.take(columns[:, :, 0, :], chosen, axis=0)
        picked = jnp.where(filled[:, None, None], picked, jnp.zeros((), columns.dtype))
        return picked.reshape(dp_count, pooled, block_rows, columns.shape[-1])

    arrived = (
        lax.all_to_all(outgoing_of(grouped_in[0]), "dp", split_axis=0, concat_axis=0, tiled=True),
        lax.all_to_all(outgoing_of(grouped_in[1]), "dp", split_axis=0, concat_axis=0, tiled=True),
        lax.all_to_all(outgoing_of(grouped_in[2]), "dp", split_axis=0, concat_axis=0, tiled=True),
    )
    source_of = all_slots // capacity
    within = all_slots % capacity
    before = jnp.sum(
        (shard_of[None, :] < shard_of[:, None]) & (source_of[None, :] == source_of[:, None]), axis=1
    )
    slot_rows = source_of * pooled + before + within

    def gather_pack(columns):
        flat = columns.reshape(dp_count * pooled, block_rows, columns.shape[-1])
        return jnp.take(flat, slot_rows, axis=0).reshape(total_rows, columns.shape[-1])

    position, alive_rows, query_tag, key_tag = row_tables(all_starts, all_live, 0, -1, block_rows)
    rotated_queries = rotate(gather_pack(arrived[0]), position, query_heads)
    rotated_keys = rotate(gather_pack(arrived[1]), position, key_heads)
    values = gather_pack(arrived[2])

    def query_block(number):
        begin_row = number * query_step
        running = attend_keys(
            initial_state(query_step, query_heads, key_heads, HEAD_DIM),
            cut_rows(rotated_queries, begin_row, query_step),
            cut_rows(query_tag, begin_row, query_step),
            begin_row + jnp.arange(query_step, dtype=jnp.int32),
            rotated_keys,
            values,
            key_tag,
            0,
            query_heads,
            key_heads,
            key_step,
        )
        return finish(
            running, cut_rows(alive_rows, begin_row, query_step), query_step, query_heads, HEAD_DIM
        )

    blocks_out = lax.map(query_block, jnp.arange(total_rows // query_step, dtype=jnp.int32))
    result = lax.all_to_all(
        blocks_out.reshape(total_rows, query_heads * HEAD_DIM),
        "seq",
        split_axis=0,
        concat_axis=1,
        tiled=True,
    )
    handed = passed_along(result, "section", 1)
    return handed[None, None]


def solution(mesh):
    placed = (
        P("section", "seq", "dp", None, None),
        P("section", "seq", "dp"),
        P("section", "dp", "seq"),
        P("section", "dp", "seq"),
        P("section", "dp", "seq"),
    )
    return jax.shard_map(
        shards,
        mesh=mesh,
        in_specs=placed,
        out_specs=P("section", "dp", "seq", None),
        check_vma=False,
    )
```

profile of v0, /device:TPU:1, one launch (start us, length us, event | category | flops | bytes accessed | tf_op | source)
XLA Modules:
  0.0 743.2 jit_solution(2661464380830729391)
XLA Ops:
  0.0 8.6 %copy.46 = bf16[1,1,6,128,4096]{3,4,2,1,0:T(8,128)(2,1)} copy(bf16[1,1,6,128,4096]{4,3,2,1,0:T(8,128)(2,1)} %param.15) | data formatting | bytes 12582912 | tf_op args[0]
  12.0 4.8 all-to-all-start.2
  18.2 17.6 %all-to-all-done.2 = bf16[6,128,4,256]{1,3,0,2:T(8,128)(2,1)S(1)} async-done(((bf16[6,128,4,256]{1,3,0,2:T(8,128)(2,1)}), bf16[6,128,4,256]{1,3,0,2:T(8,128)(2,1)S(1)}, u32[]{:S(2)}, u32[]{:S(2)}) %all-to-all-start.2) | async-done | bytes 1572896 | tf_op jit(solution)/shard_map/all_to_all | solution.py:220
  44.8 12.5 %all-to-all-done.4 = bf16[6,128,4,256]{1,3,0,2:T(8,128)(2,1)S(1)} async-done(((bf16[6,128,4,256]{1,3,0,2:T(8,128)(2,1)}), bf16[6,128,4,256]{1,3,0,2:T(8,128)(2,1)S(1)}, u32[]{:S(2)}, u32[]{:S(2)}) %all-to-all-start.4) | async-done | bytes 1572896 | tf_op jit(solution)/shard_map/all_to_all | solution.py:219
  62.8 35.8 %all-reduce.4 = (s32[24]{0:T(128)S(1)}, s32[24]{0:T(128)S(1)}, s32[24]{0:T(128)S(1)}, s32[24]{0:T(128)S(1)}) all-reduce(s32[24]{0:T(128)S(1)} %bitcast_dynamic-update-slice_fusion.3, s32[24]{0:T(128)S(1)} %bitcast_dynamic-update-slice_fusion.2, ...), channel_id=2, replica_groups=mesh['dp'=16,'seq'=4,'section'=4] {'seq'}, use_global_device_ids=true, to_apply=%add | all-reduce | flops 96 | bytes 768
  115.9 66.4 %all_to_all.79 = bf16[16,2,128,256]{3,2,1,0:T(8,128)(2,1)} all-to-all(bf16[16,2,128,256]{3,2,1,0:T(8,128)(2,1)} %bitcast.134), channel_id=1, replica_groups=mesh['dp'=16,'seq'=4,'section'=4] {'dp'}, dimensions={0} | all-to-all | bytes 4194304 | tf_op jit(solution)/shard_map/all_to_all | solution.py:240
  197.6 36.7 %all-to-all-done.5 = bf16[16,2,128,256]{3,2,1,0:T(8,128)(2,1)} async-done(((bf16[16,2,128,256]{3,2,1,0:T(8,128)(2,1)}), bf16[16,2,128,256]{3,2,1,0:T(8,128)(2,1)}, u32[]{:S(2)}, u32[]{:S(2)}) %all-to-all-start.5) | async-done | bytes 2097184 | tf_op jit(solution)/shard_map/all_to_all | solution.py:239
  234.3 5.1 all-to-all-start.1
  240.3 7.0 multiply_cosine_fusion.1
  258.1 6.9 fusion.28
  266.4 66.6 %all-to-all-done.1 = bf16[16,2,128,512]{3,2,1,0:T(8,128)(2,1)} async-done(((bf16[16,2,128,512]{3,2,1,0:T(8,128)(2,1)}), bf16[16,2,128,512]{3,2,1,0:T(8,128)(2,1)}, u32[]{:S(2)}, u32[]{:S(2)}) %all-to-all-start.1) | async-done | bytes 4194336 | tf_op jit(solution)/shard_map/all_to_all | solution.py:238
  337.6 5.5 gather.21
  343.1 12.4 %fusion.22 = f32[3072,2,256]{2,1,0:T(2,128)S(1)} fusion(bf16[3072,2,256]{2,1,0:T(2,128)(2,1)} %gather.21, pred[3072]{0:T(1024)(128)(4,1)S(1)} %broadcast_bitcast_fusion), kind=kLoop, calls=%fused_computation.41 | loop fusion | flops 3145728 | bytes 9440256 | tf_op jit(solution)/shard_map/convert_element_type | solution.py:29
  355.5 8.3 %subtract_convert_fusion = (bf16[3072,2,128]{2,1,0:T(2,128)(2,1)S(1)}, bf16[3072,2,128]{2,1,0:T(2,128)(2,1)S(1)}) fusion(f32[3072,2,256]{2,1,0:T(2,128)S(1)} %fusion.22, f32[3072,128]{1,0:T(8,128)S(1)} %copy-done.5, f32[3072,128]{1,0:T(8,128)S(1)} %copy-done.4), kind=kLoop, calls=%fused_computation.44 | loop fusion | flops 6291456 | bytes 12582912 | tf_op jit(solution)/shard_map/convert.3
  369.5 254.5 %while.26 = (s32[]{:T(128)}, bf16[6,512,512]{2,1,0:T(8,128)(2,1)}, s32[6]{0:T(128)S(1)}, pred[3072]{0:T(1024)(128)(4,1)S(1)}, f32[3072]{0:T(1024)S(1)}, /*index=...) while((s32[]{:T(128)}, bf16[6,512,512]{2,1,0:T(8,128)(2,1)}, ...), condition=%wide.region_13.16_spmd.clone, body=%wide.region_6.15_spmd.clone.sunk | while | flops 271330304 | bytes 10019224 | solution.py:277
  372.0 37.0 %while.27 = (s32[]{:T(128)}, f32[512,1,2,256]{0,3,2,1:T(8,128)S(1)}, f32[512,1,2]{0,2,1:T(2,128)S(1)}, f32[512]{0:T(512)S(1)}, s32[12]{0:T(128)S(1)}, /*index=5*...) while((s32[]{:T(128)}, ...), condition=%wide.region_12.14_spmd.clone, body=%wide.region_7.13_spmd.clone.sunk | while | flops 270533632 | bytes 4222261 | solution.py:150
  412.9 40.8 %while.27 = (s32[]{:T(128)}, f32[512,1,2,256]{0,3,2,1:T(8,128)S(1)}, f32[512,1,2]{0,2,1:T(2,128)S(1)}, f32[512]{0:T(512)S(1)}, s32[12]{0:T(128)S(1)}, /*index=5*...) while((s32[]{:T(128)}, ...), condition=%wide.region_12.14_spmd.clone, body=%wide.region_7.13_spmd.clone.sunk | while | flops 270533632 | bytes 4222261 | solution.py:150
  457.5 37.0 %while.27 = (s32[]{:T(128)}, f32[512,1,2,256]{0,3,2,1:T(8,128)S(1)}, f32[512,1,2]{0,2,1:T(2,128)S(1)}, f32[512]{0:T(512)S(1)}, s32[12]{0:T(128)S(1)}, /*index=5*...) while((s32[]{:T(128)}, ...), condition=%wide.region_12.14_spmd.clone, body=%wide.region_7.13_spmd.clone.sunk | while | flops 270533632 | bytes 4222261 | solution.py:150
  498.3 38.9 %while.27 = (s32[]{:T(128)}, f32[512,1,2,256]{0,3,2,1:T(8,128)S(1)}, f32[512,1,2]{0,2,1:T(2,128)S(1)}, f32[512]{0:T(512)S(1)}, s32[12]{0:T(128)S(1)}, /*index=5*...) while((s32[]{:T(128)}, ...), condition=%wide.region_12.14_spmd.clone, body=%wide.region_7.13_spmd.clone.sunk | while | flops 270533632 | bytes 4222261 | solution.py:150
  541.0 40.8 %while.27 = (s32[]{:T(128)}, f32[512,1,2,256]{0,3,2,1:T(8,128)S(1)}, f32[512,1,2]{0,2,1:T(2,128)S(1)}, f32[512]{0:T(512)S(1)}, s32[12]{0:T(128)S(1)}, /*index=5*...) while((s32[]{:T(128)}, ...), condition=%wide.region_12.14_spmd.clone, body=%wide.region_7.13_spmd.clone.sunk | while | flops 270533632 | bytes 4222261 | solution.py:150
  585.6 37.0 %while.27 = (s32[]{:T(128)}, f32[512,1,2,256]{0,3,2,1:T(8,128)S(1)}, f32[512,1,2]{0,2,1:T(2,128)S(1)}, f32[512]{0:T(512)S(1)}, s32[12]{0:T(128)S(1)}, /*index=5*...) while((s32[]{:T(128)}, ...), condition=%wide.region_12.14_spmd.clone, body=%wide.region_7.13_spmd.clone.sunk | while | flops 270533632 | bytes 4222261 | solution.py:150
  624.0 38.2 %all_to_all.80 = bf16[4,768,512]{2,1,0:T(8,128)(2,1)S(1)} all-to-all(bf16[4,768,512]{2,1,0:T(8,128)(2,1)} %bitcast.139), channel_id=1, replica_groups=mesh['dp'=16,'seq'=4,'section'=4] {'seq'}, dimensions={0} | all-to-all | bytes 6291456 | tf_op jit(solution)/shard_map/all_to_all | solution.py:278
  664.9 7.9 %collective-permute-start = (bf16[768,2048]{0,1:T(8,128)(2,1)}, bf16[768,2048]{0,1:T(8,128)(2,1)S(1)}, u32[]{:S(2)}, u32[]{:S(2)}) collective-permute-start(bf16[768,2048]{0,1:T(8,128)(2,1)} %bitcast.140), channel_id=1, source_target_pairs={{3,0},{0,1},{1,2},{2,3},{7,4},{4,5},{5,6},{6,7},{11,8},{8,9},{9,10... | collective-permute-start | bytes 9437192 | tf_op jit(solution)/shard_map/ppermute | solution.py:18
  672.8 67.5 %collective-permute-done = bf16[768,2048]{0,1:T(8,128)(2,1)S(1)} collective-permute-done((bf16[768,2048]{0,1:T(8,128)(2,1)}, bf16[768,2048]{0,1:T(8,128)(2,1)S(1)}, u32[]{:S(2)}, u32[]{:S(2)}) %collective-permute-start) | collective-permute-done | bytes 3145760 | tf_op jit(solution)/shard_map/ppermute | solution.py:18
  (647 shorter events, 272.9 us)
Async XLA Ops:
  12.0 23.7 %all-to-all-start.2 = ((bf16[6,128,4,256]{1,3,0,2:T(8,128)(2,1)}), bf16[6,128,4,256]{1,3,0,2:T(8,128)(2,1)S(1)}, u32[]{:S(2)}, u32[]{:S(2)}) async-start(bf16[6,128,4,256]{1,3,0,2:T(8,128)(2,1)} %copy.50), calls=%async_computation.2 | async-start | bytes 3145728 | tf_op jit(solution)/shard_map/all_to_all | solution.py:220
  35.7 5.7 copy-start.2
  35.7 21.6 %all-to-all-start.4 = ((bf16[6,128,4,256]{1,3,0,2:T(8,128)(2,1)}), bf16[6,128,4,256]{1,3,0,2:T(8,128)(2,1)S(1)}, u32[]{:S(2)}, u32[]{:S(2)}) async-start(bf16[6,128,4,256]{1,3,0,2:T(8,128)(2,1)} %copy.52), calls=%async_computation.4 | async-start | bytes 3145728 | tf_op jit(solution)/shard_map/all_to_all | solution.py:219
  41.4 2.0 copy-start.11
  44.8 17.5 %copy-start.7 = (s32[1,1,6]{2,1,0:T(1,128)S(1)}, s32[1,1,6]{2,1,0:T(1,128)}, u32[]{:S(2)}) copy-start(s32[1,1,6]{2,1,0:T(1,128)} %param.16) | copy-start | bytes 76
  44.8 17.7 %copy-start.8 = (s32[1,1,6]{2,1,0:T(1,128)S(1)}, s32[1,1,6]{2,1,0:T(1,128)}, u32[]{:S(2)}) copy-start(s32[1,1,6]{2,1,0:T(1,128)} %param.17) | copy-start | bytes 76
  44.8 17.8 %copy-start.9 = (s32[1,1,6]{2,1,0:T(1,128)S(1)}, s32[1,1,6]{2,1,0:T(1,128)}, u32[]{:S(2)}) copy-start(s32[1,1,6]{2,1,0:T(1,128)} %param.18) | copy-start | bytes 76
  44.8 17.9 %copy-start.10 = (s32[1,1,6]{2,1,0:T(1,128)S(1)}, s32[1,1,6]{2,1,0:T(1,128)}, u32[]{:S(2)}) copy-start(s32[1,1,6]{2,1,0:T(1,128)} %param.19) | copy-start | bytes 76
  57.3 1.2 copy-start.3
  58.6 57.4 %all-to-all-start = ((bf16[6,128,4,512]{1,3,0,2:T(8,128)(2,1)}), bf16[6,128,4,512]{1,3,0,2:T(8,128)(2,1)S(1)}, u32[]{:S(2)}, u32[]{:S(2)}) async-start(bf16[6,128,4,512]{1,3,0,2:T(8,128)(2,1)} %copy.47), calls=%async_computation | async-start | bytes 6291456 | tf_op jit(solution)/shard_map/all_to_all | solution.py:218
  115.9 66.5 %copy-start = (bf16[6,128,4,512]{1,3,0,2:T(8,128)(2,1)}, bf16[6,128,4,512]{1,3,0,2:T(8,128)(2,1)S(1)}, u32[]{:S(2)}) copy-start(bf16[6,128,4,512]{1,3,0,2:T(8,128)(2,1)S(1)} %all-to-all-done) | copy-start | bytes 9437188
  182.4 51.9 %all-to-all-start.5 = ((bf16[16,2,128,256]{3,2,1,0:T(8,128)(2,1)}), bf16[16,2,128,256]{3,2,1,0:T(8,128)(2,1)}, u32[]{:S(2)}, u32[]{:S(2)}) async-start(bf16[16,2,128,256]{3,2,1,0:T(8,128)(2,1)} %bitcast.133), calls=%async_computation.5 | async-start | bytes 4194304 | tf_op jit(solution)/shard_map/all_to_all | solution.py:239
  234.3 98.6 %all-to-all-start.1 = ((bf16[16,2,128,512]{3,2,1,0:T(8,128)(2,1)}), bf16[16,2,128,512]{3,2,1,0:T(8,128)(2,1)}, u32[]{:S(2)}, u32[]{:S(2)}) async-start(bf16[16,2,128,512]{3,2,1,0:T(8,128)(2,1)} %select_select_fusion), calls=%async_computation.1 | async-start | bytes 8388608 | tf_op jit(solution)/shard_map/all_to_all | solution.py:238
  239.4 7.9 %copy-start.1 = (bf16[16,2,128,256]{3,2,1,0:T(8,128)(2,1)S(1)}, bf16[16,2,128,256]{3,2,1,0:T(8,128)(2,1)}, u32[]{:S(2)}) copy-start(bf16[16,2,128,256]{3,2,1,0:T(8,128)(2,1)} %all_to_all.79) | copy-start | bytes 6291460
  249.1 3.6 copy-start.6
  343.1 12.4 %copy-start.4 = (f32[3072,128]{1,0:T(8,128)S(1)}, f32[3072,128]{1,0:T(8,128)}, u32[]{:S(2)}) copy-start(f32[3072,128]{1,0:T(8,128)} %get-tuple-element.330) | copy-start | bytes 4718596
  343.1 12.4 %copy-start.5 = (f32[3072,128]{1,0:T(8,128)S(1)}, f32[3072,128]{1,0:T(8,128)}, u32[]{:S(2)}) copy-start(f32[3072,128]{1,0:T(8,128)} %get-tuple-element.331) | copy-start | bytes 4718596
  664.9 75.4 %collective-permute-start = (bf16[768,2048]{0,1:T(8,128)(2,1)}, bf16[768,2048]{0,1:T(8,128)(2,1)S(1)}, u32[]{:S(2)}, u32[]{:S(2)}) collective-permute-start(bf16[768,2048]{0,1:T(8,128)(2,1)} %bitcast.140), channel_id=1, source_target_pairs={{3,0},{0,1},{1,2},{2,3},{7,4},{4,5},{5,6},{6,7},{11,8},{8,9},{9,10... | collective-permute-start | bytes 9437192 | tf_op jit(solution)/shard_map/ppermute | solution.py:18
where the time goes:
time: 753 us; the launch traced here: 743 us
  waiting for transfers between devices  201 us (27%)
  blocking collectives  140 us (19%)
  local copies, waits for them, and re-layouts  123 us (16%)
  other arithmetic  123 us (16%)
  loops' own time  94.3 us (13%)
  matrix products  31.4 us (4%)
  starting transfers between devices  29.5 us (4%)
    another operation x6, loops' own time, attend_keys(): lax.scan(key_turn, running, jnp.arange(key_rows.shape[0] // key_step, dty...  89.3 us
    ppermute x1, waiting for transfers between devices, passed_along(): return lax.ppermute(block, axis, route)  67.5 us
    all_to_all x1, waiting for transfers between devices, shards(): lax.all_to_all(outgoing_of(grouped_in[0]), 'dp', split_axis=0, concat_axi...  66.6 us
    all_to_all x1, blocking collectives, shards(): lax.all_to_all(outgoing_of(grouped_in[2]), 'dp', split_axis=0, concat_axi...  66.4 us
    reduce_or x72, other arithmetic, attend(): return lax.cond(jnp.any(allowed), compute, keep, running)  60.9 us
    dynamic_slice x72, local copies, waits for them, and re-layouts, attend_keys(): lax.scan(key_turn, running, jnp.arange(key_rows.shape[0] // key_step, dty...  42.4 us
    all_to_all x1, blocking collectives, shards(): lax.all_to_all(blocks_out.reshape(total_rows, query_heads * HEAD_DIM), 's...  38.2 us
    all_to_all x1, waiting for transfers between devices, shards(): lax.all_to_all(outgoing_of(grouped_in[1]), 'dp', split_axis=0, concat_axi...  36.7 us
  transfers between devices with their start and end apart: 6, of which 5 were waited for; matrix products, arithmetic and copies ran while one was open for 8% of the time, Pallas kernels for 0%

commit v1 on v0

v1 whole, which is shorter than its diff:
```python
import jax
import jax.numpy as jnp
from jax import lax
from jax.experimental import pallas as pl
from jax.experimental.pallas import tpu as pltpu
from jax.sharding import PartitionSpec as P


HEADS = 8
KV_HEADS = 4
HEAD_DIM = 256
BLOCK = 128
DOC_MOST = 8

SCORE_CAP = 50.0
ROPE_BASE = 10000.0
LOG2_E = 1.4426950408889634


VMEM = pltpu.VMEM
SMEM = pltpu.SMEM


def whole(space):
    return pl.BlockSpec(memory_space=space)


def seq_shift(array, distance):
    n = lax.axis_size("seq")
    return lax.ppermute(array, "seq", [(i, (i + distance) % n) for i in range(n)])


def section_shift(array):
    n = lax.axis_size("section")
    return lax.ppermute(array, "section", [(i, (i + 1) % n) for i in range(n)])


def both_shift(array, distance):
    m, n = lax.axis_size("section"), lax.axis_size("seq")
    route = [
        (s * m + t, ((s + distance) % n) * m + (t + 1) % m) for s in range(n) for t in range(m)
    ]
    return lax.ppermute(array, ("seq", "section"), route)


def cost(flops, bytes_accessed, transcendentals=0):
    return pl.CostEstimate(
        flops=int(flops), bytes_accessed=int(bytes_accessed), transcendentals=int(transcendentals)
    )


def outgoing(chosen, groups):
    slots = chosen.shape[0]
    rows, width = groups[0][0].shape
    blocks = rows // BLOCK
    pieces = len(groups[0])
    total = width * len(groups)

    def kernel(chosen_ref, *refs):
        out_ref = refs[-1]

        def slot(i, carry):
            pick = chosen_ref[i]
            piece = pick // blocks
            start = pl.multiple_of((pick % blocks) * BLOCK, BLOCK)
            for d in range(pieces):

                @pl.when(piece == d)
                def _():
                    for g in range(len(groups)):
                        out_ref[i, :, g * width : (g + 1) * width] = refs[g * pieces + d][
                            pl.ds(start, BLOCK), :
                        ]

            return carry

        lax.fori_loop(0, slots, slot, 0)

    flat = [piece for group in groups for piece in group]
    moved = 2 * BLOCK * total * (slots + blocks * pieces)
    return pl.pallas_call(
        kernel,
        out_shape=jax.ShapeDtypeStruct((slots, BLOCK, total), flat[0].dtype),
        in_specs=[whole(SMEM)] + [whole(VMEM)] * len(flat),
        out_specs=whole(VMEM),
        cost_estimate=cost(3e6, moved),
    )(chosen, *flat)


def turned(block, cosine, sine):
    half = HEAD_DIM // 2
    first = block[:, :half].astype(jnp.float32)
    second = block[:, half:].astype(jnp.float32)
    return jnp.concatenate(
        [first * cosine - second * sine, second * cosine + first * sine], axis=1
    ).astype(jnp.bfloat16)


def pack_keys(slot_rows, offset, arrived, cosine, sine):
    count = slot_rows.shape[0]

    def kernel(slot_ref, offset_ref, arrived_ref, cos_ref, sin_ref, out_ref):
        def block(p, carry):
            at = pl.multiple_of(offset_ref[p] * BLOCK, BLOCK)
            to = pl.multiple_of(p * BLOCK, BLOCK)
            out_ref[pl.ds(to, BLOCK), :] = turned(
                arrived_ref[slot_ref[p]], cos_ref[pl.ds(at, BLOCK), :], sin_ref[pl.ds(at, BLOCK), :]
            )
            return carry

        lax.fori_loop(0, count, block, 0)

    return pl.pallas_call(
        kernel,
        out_shape=jax.ShapeDtypeStruct((count * BLOCK, HEAD_DIM), arrived.dtype),
        in_specs=[whole(SMEM)] * 2 + [whole(VMEM)] * 3,
        out_specs=whole(VMEM),
        cost_estimate=cost(1e7, 5e6),
        name="pack_keys",
    )(slot_rows, offset, arrived, cosine, sine)


def attend(tables, shard, queries, query_column, keys, arrived, cosine, sine, blocks):
    count = keys.shape[0] // BLOCK
    window = DOC_MOST - 1 + blocks
    most_pairs = DOC_MOST // 2
    arg_scale = HEAD_DIM**-0.5 / SCORE_CAP
    exp_scale = SCORE_CAP * LOG2_E

    def kernel(
        table_ref, shard_ref, q_ref, k_ref, v_ref, cos_ref, sin_ref, out_ref,
        q_buf, k_buf, v_buf, cos_buf, sin_buf, q_sems, v_sems, sems,
    ):
        begin = shard_ref[0] * blocks
        low = jnp.clip(begin - (DOC_MOST - 1), 0, count - window)
        copies = [
            pltpu.make_async_copy(
                k_ref.at[pl.ds(pl.multiple_of(low * BLOCK, BLOCK), window * BLOCK), :],
                k_buf,
                sems.at[0],
            ),
            pltpu.make_async_copy(cos_ref, cos_buf, sems.at[1]),
            pltpu.make_async_copy(sin_ref, sin_buf, sems.at[2]),
        ]
        for i in range(blocks):
            copies.append(
                pltpu.make_async_copy(
                    q_ref.at[table_ref[0, begin + i], :, pl.ds(query_column, HEAD_DIM)],
                    q_buf.at[i],
                    q_sems.at[i],
                )
            )
        for i in range(window):
            copies.append(
                pltpu.make_async_copy(
                    v_ref.at[table_ref[0, low + i], :, pl.ds(0, HEAD_DIM)],
                    v_buf.at[pl.ds(i * BLOCK, BLOCK), :],
                    v_sems.at[i],
                )
            )
        for copy in copies:
            copy.start()
        row = lax.broadcasted_iota(jnp.int32, (BLOCK, BLOCK), 0)
        col = lax.broadcasted_iota(jnp.int32, (BLOCK, BLOCK), 1)
        ahead = col - row
        row_of = lax.broadcasted_iota(jnp.int32, (BLOCK, HEAD_DIM), 0)
        for copy in copies:
            copy.wait()

        def block(i, carry):
            p = begin + i
            at = pl.multiple_of(table_ref[1, p] * BLOCK, BLOCK)
            first = table_ref[2, p]
            live = table_ref[3, p]
            query = turned(
                q_buf[i], cos_buf[pl.ds(at, BLOCK), :], sin_buf[pl.ds(at, BLOCK), :]
            )
            pairs = (p - first + 2) // 2
            to = pl.multiple_of(i * BLOCK, BLOCK)
            for n in range(1, most_pairs + 1):

                @pl.when(pairs == n)
                def _(n=n):
                    base = jnp.minimum(first, low + window - 2 * n)
                    start = pl.multiple_of((base - low) * BLOCK, BLOCK)
                    scores = lax.dot_general(
                        query,
                        k_buf[pl.ds(start, 2 * n * BLOCK), :],
                        (((1,), (1,)), ((), ())),
                        preferred_element_type=jnp.float32,
                    )
                    total = jnp.zeros((BLOCK, BLOCK), jnp.float32)
                    rounded = []
                    for k in range(2 * n):
                        key_block = base + k
                        limit = jnp.where(key_block >= first, table_ref[3, key_block], 0)
                        allowed = (col < limit) & (ahead <= (p - key_block) * BLOCK)
                        part = scores[:, k * BLOCK : (k + 1) * BLOCK]
                        weight = jnp.where(
                            allowed, jnp.exp2(jnp.tanh(part * arg_scale) * exp_scale), 0.0
                        )
                        total = total + weight
                        rounded.append(weight.astype(jnp.bfloat16))
                    numerator = lax.dot_general(
                        jnp.concatenate(rounded, axis=1),
                        v_buf[pl.ds(start, 2 * n * BLOCK), :],
                        (((1,), (0,)), ((), ())),
                        preferred_element_type=jnp.float32,
                    )
                    alive = row_of < live
                    summed = jnp.sum(total, axis=1, keepdims=True)
                    safe = jnp.where(alive[:, :1], summed, 1.0)
                    out_ref[pl.ds(to, BLOCK), :] = jnp.where(
                        alive, numerator / safe, 0.0
                    ).astype(jnp.bfloat16)

            return carry

        lax.fori_loop(0, blocks, block, 0)

    pairs = blocks * DOC_MOST / 2
    trig = (DOC_MOST * BLOCK, HEAD_DIM // 2)
    return pl.pallas_call(
        kernel,
        out_shape=jax.ShapeDtypeStruct((blocks * BLOCK, HEAD_DIM), keys.dtype),
        in_specs=[whole(SMEM)] * 2 + [whole(pl.ANY)] * 5,
        out_specs=whole(VMEM),
        scratch_shapes=[
            VMEM((blocks, BLOCK, HEAD_DIM), jnp.bfloat16),
            VMEM((window * BLOCK, HEAD_DIM), jnp.bfloat16),
            VMEM((window * BLOCK, HEAD_DIM), jnp.bfloat16),
            VMEM(trig, jnp.float32),
            VMEM(trig, jnp.float32),
            pltpu.SemaphoreType.DMA((blocks,)),
            pltpu.SemaphoreType.DMA((window,)),
            pltpu.SemaphoreType.DMA((3,)),
        ],
        cost_estimate=cost(
            pairs * 4 * BLOCK * BLOCK * HEAD_DIM, 4e6, pairs * 2 * BLOCK * BLOCK
        ),
        name="attend",
    )(tables, shard, queries, keys, arrived, cosine, sine)


def assemble(columns, pieces):
    rows, width = pieces[0].shape
    count = len(pieces)

    def kernel(column_ref, *refs):
        out_ref, sems = refs[count], refs[count + 1]
        copies = []
        for n in range(count):
            at = pl.multiple_of(column_ref[n] * width, width)
            copy = pltpu.make_async_copy(refs[n], out_ref.at[:, pl.ds(at, width)], sems.at[n])
            copy.start()
            copies.append(copy)
        for copy in copies:
            copy.wait()

    return pl.pallas_call(
        kernel,
        out_shape=jax.ShapeDtypeStruct((rows, width * count), pieces[0].dtype),
        in_specs=[whole(SMEM)] + [whole(VMEM)] * count,
        out_specs=whole(pl.ANY),
        scratch_shapes=[pltpu.SemaphoreType.DMA((count,))],
        cost_estimate=cost(1e6, 4 * rows * width * count),
        name="assemble",
    )(columns, *pieces)


def send_plan(owners, shard_count, blocks, me, pooled, dp_count):
    total = owners.shape[0]
    index = jnp.arange(total, dtype=jnp.int32)
    same = (owners[:, None] == owners[None, :]) & (index[None, :] < index[:, None])
    target = owners * pooled + jnp.sum(same, axis=1, dtype=jnp.int32)
    slots = jnp.arange(dp_count * pooled, dtype=jnp.int32)
    matches = target[None, :] == slots[:, None]
    distance = (me - index // blocks) % shard_count
    place = distance * blocks + index % blocks
    return jnp.sum(jnp.where(matches, place[None, :], 0), axis=1, dtype=jnp.int32)


def arrival_plan(slots, shard_of, capacity, pooled):
    source = slots // capacity
    before = jnp.sum(
        (shard_of[None, :] < shard_of[:, None]) & (source[None, :] == source[:, None]),
        axis=1,
        dtype=jnp.int32,
    )
    return source * pooled + before + slots % capacity


def shards(projected, dest_owner, slot_from, doc_starts, live_rows):
    source_blocks, block_rows, full_width = projected.shape[2:]
    rows = source_blocks * block_rows
    source = projected.reshape(rows, full_width)
    dp_count = lax.axis_size("dp")
    seq_count = lax.axis_size("seq")
    capacity = (source_blocks + dp_count - 1) // dp_count
    total_blocks = seq_count * source_blocks
    pooled = (total_blocks + dp_count - 1) // dp_count
    group = HEADS // KV_HEADS
    query_width = HEADS * HEAD_DIM
    key_width = KV_HEADS * HEAD_DIM
    me = lax.axis_index("seq")
    distances = range(seq_count)

    def part(base, stride, distance):
        at = base + ((me + distance) % seq_count) * stride
        return lax.dynamic_slice_in_dim(source, at, HEAD_DIM, 1)

    mine = jnp.stack([dest_owner[0, 0], slot_from[0, 0], doc_starts[0, 0], live_rows[0, 0]])
    before = section_shift(mine)
    pair = jnp.stack([mine, before])
    key_pieces, pairs, value_pieces = [], [], []
    query_pieces = [[] for _ in range(group)]
    for d in distances:
        piece = part(query_width, HEAD_DIM, d)
        key_pieces.append(seq_shift(piece, d) if d else piece)
        pairs.append(seq_shift(pair, d) if d else pair)
        value_pieces.append(both_shift(part(query_width + key_width, HEAD_DIM, d), d))
        for h in range(group):
            query_pieces[h].append(
                both_shift(part(h * HEAD_DIM, group * HEAD_DIM, d), d)
            )
    tables = jnp.stack(pairs)[(me - jnp.arange(seq_count, dtype=jnp.int32)) % seq_count]
    tables = tables.transpose(1, 2, 0, 3).reshape(2, 4, total_blocks)

    shard_of = jnp.repeat(jnp.arange(seq_count, dtype=jnp.int32), source_blocks)
    block_ids = jnp.arange(total_blocks, dtype=jnp.int32)

    def plans(tables):
        chosen = send_plan(tables[0], seq_count, source_blocks, me, pooled, dp_count)
        slot_rows = arrival_plan(tables[1], shard_of, capacity, pooled)
        first = lax.cummax(jnp.where(tables[2] == 1, block_ids, -1), axis=0)
        return chosen, jnp.stack([slot_rows, block_ids - first, first, tables[3]])

    chosen_here, plan_here = plans(tables[0])
    chosen_there, plan_there = plans(tables[1])

    def exchange(chosen, groups):
        sent = outgoing(chosen, groups)
        width = sent.shape[-1]
        sent = sent.reshape(dp_count, pooled, block_rows, width)
        got = lax.all_to_all(sent, "dp", split_axis=0, concat_axis=0, tiled=True)
        return got.reshape(dp_count * pooled, block_rows, width)

    frequency = ROPE_BASE ** (
        -2.0 * jnp.arange(HEAD_DIM // 2, dtype=jnp.float32) / HEAD_DIM
    )
    positions = jnp.arange(DOC_MOST * block_rows, dtype=jnp.float32)
    angles = positions[:, None] * frequency[None, :]
    cosine, sine = jnp.cos(angles), jnp.sin(angles)

    key_arrived = exchange(chosen_here, [key_pieces])
    value_arrived = exchange(chosen_there, [value_pieces, query_pieces[0]])
    query_arrived = exchange(chosen_there, [query_pieces[1]])
    keys = section_shift(pack_keys(plan_here[0], plan_here[1], key_arrived, cosine, sine))

    pieces, columns = [], []
    for h, (queries, column) in enumerate([(value_arrived, HEAD_DIM), (query_arrived, 0)]):
        for d in [2, 1, 3, 0]:
            shard = ((me + d) % seq_count).astype(jnp.int32).reshape(1)
            out = attend(
                plan_there, shard, queries, column, keys, value_arrived, cosine, sine,
                source_blocks,
            )
            pieces.append(out if d == 0 else seq_shift(out, d))
            columns.append(((me - d) % seq_count) * group + h)
    result = assemble(jnp.stack(columns).astype(jnp.int32), pieces)
    return result[None, None]


def solution(mesh):
    placed = (
        P("section", "seq", "dp", None, None),
        P("section", "seq", "dp"),
        P("section", "dp", "seq"),
        P("section", "dp", "seq"),
        P("section", "dp", "seq"),
    )

    return jax.shard_map(
        shards,
        mesh=mesh,
        in_specs=placed,
        out_specs=P("section", "dp", "seq", None),
        check_vma=False,
    )
```

time: 753 us -> 342 us (0.45); the launches traced: 743 us -> 340 us
  blocking collectives: 140 us -> 0 us
  other arithmetic: 123 us -> 6.39 us
  local copies, waits for them, and re-layouts: 123 us -> 13.8 us
  loops' own time: 94.3 us -> 0 us
  Pallas kernels: 0 us -> 70.9 us
  matrix products: 31.4 us -> 0 us
  starting transfers between devices: 29.5 us -> 56.8 us
  waiting for transfers between devices: 201 us -> 192 us
    all_to_all x2 -> x0, blocking collectives: 105 us -> none  [the longest x1 66.4 us: shards(): lax.all_to_all(outgoing_of(grouped_in[2]), 'dp', split_axis=0, concat_axi...]
    another operation x79 -> x0, loops' own time: 94.3 us -> none  [the longest x6 89.3 us: attend_keys(): lax.scan(key_turn, running, jnp.arange(key_rows.shape[0] // key_step, dty...]
    all_to_all x5 -> x3, waiting for transfers between devices: 133 us -> 50.5 us  [exchange(): got = lax.all_to_all(sent, 'dp', split_axis=0, concat_axis=0, tiled=True)]
    ppermute x1 -> x26, waiting for transfers between devices: 67.5 us -> 142 us  [the longest x12 91.8 us: both_shift(): return lax.ppermute(array, ('seq', 'section'), route)]
    pallas_call x0 -> x13, Pallas kernels: none -> 70.9 us  [the longest x8 50.3 us: attend(): pl.pallas_call(kernel, out_shape=jax.ShapeDtypeStruct((blocks * BLOCK, HE...]
    reduce_or x73 -> x0, other arithmetic: 61 us -> none  [the longest x72 60.9 us: attend(): return lax.cond(jnp.any(allowed), compute, keep, running)]
    dynamic_slice x96 -> x1, local copies, waits for them, and re-layouts: 53.3 us -> 4.78 us  [part(): return lax.dynamic_slice_in_dim(source, at, HEAD_DIM, 1)]
    unnamed x1 -> x0, blocking collectives: 35.8 us -> none
  transfers between devices with their start and end apart: 6 -> 29, of which waited for: 5 -> 7; matrix products, arithmetic and copies ran while one was open for 8% -> 4% of each run, Pallas kernels for 0% -> 19%
where the time goes in v1:
time: 342 us; the launch traced here: 340 us
  waiting for transfers between devices  192 us (56%)
  Pallas kernels  70.9 us (21%)
  starting transfers between devices  56.8 us (17%)
  local copies, waits for them, and re-layouts  13.8 us (4%)
  other arithmetic  6.39 us (2%)
    ppermute x12, waiting for transfers between devices, both_shift(): return lax.ppermute(array, ('seq', 'section'), route)  91.8 us
    all_to_all x3, waiting for transfers between devices, exchange(): got = lax.all_to_all(sent, 'dp', split_axis=0, concat_axis=0, tiled=True)  50.5 us
    pallas_call x8, Pallas kernels, attend(): pl.pallas_call(kernel, out_shape=jax.ShapeDtypeStruct((blocks * BLOCK, HE...  50.3 us
    ppermute x2, waiting for transfers between devices, section_shift(): return lax.ppermute(array, 'section', [(i, (i + 1) % n) for i in range(n)])  36.2 us
    all_to_all x3, starting transfers between devices, exchange(): got = lax.all_to_all(sent, 'dp', split_axis=0, concat_axis=0, tiled=True)  23.7 us
    ppermute x12, starting transfers between devices, both_shift(): return lax.ppermute(array, ('seq', 'section'), route)  16.5 us
    ppermute x12, starting transfers between devices, seq_shift(): lax.ppermute(array, 'seq', [(i, (i + distance) % n) for i in range(n)])  14.4 us
    ppermute x12, waiting for transfers between devices, seq_shift(): lax.ppermute(array, 'seq', [(i, (i + distance) % n) for i in range(n)])  13.7 us
  transfers between devices with their start and end apart: 29, of which 7 were waited for; matrix products, arithmetic and copies ran while one was open for 4% of the time, Pallas kernels for 19%

profile of v1, /device:TPU:1, one launch (start us, length us, event | category | flops | bytes accessed | tf_op | source)
XLA Modules:
  0.0 340.4 jit_solution(193882137437794679)
XLA Ops:
  2.9 4.8 %constant_dynamic-slice_fusion = (bf16[768,256]{1,0:T(8,128)(2,1)S(1)}, bf16[768,256]{1,0:T(8,128)(2,1)S(1)}, bf16[768,256]{1,0:T(8,128)(2,1)S(1)}, bf16[768,256...) fusion(bf16[768,4096]{1,0:T(8,128)(2,1)} %bitcast.43, ...), kind=kLoop, calls=%fused_computation.22 | loop fusion | bytes 12582976 | tf_op jit(solution)/shard_map/dynamic_slice | solution.py:310
  13.3 5.4 %collective-permute-done.3 = s32[2,4,6]{2,1,0:T(4,128)S(1)} collective-permute-done((s32[2,4,6]{2,1,0:T(4,128)S(1)}, s32[2,4,6]{2,1,0:T(4,128)S(1)}, u32[]{:S(2)}, u32[]{:S(2)}) %collective-permute-start.3) | collective-permute-done | bytes 224 | tf_op jit(solution)/shard_map/ppermute | solution.py:30
  19.9 8.3 %collective-permute-done.2 = s32[2,4,6]{2,1,0:T(4,128)S(1)} collective-permute-done((s32[2,4,6]{2,1,0:T(4,128)S(1)}, s32[2,4,6]{2,1,0:T(4,128)S(1)}, u32[]{:S(2)}, u32[]{:S(2)}) %collective-permute-start.2) | collective-permute-done | bytes 224 | tf_op jit(solution)/shard_map/ppermute | solution.py:30
  30.9 4.0 %shard_map.56 = bf16[32,128,256]{2,1,0:T(8,128)(2,1)} custom-call(s32[32]{0:T(128)} %get-tuple-element.13.chosen_ref, bf16[768,256]{1,0:T(8,128)(2,1)} %get-tuple-element.24.refs_0_, bf16[768,256]{1,0:T(8,128)(2,1)} %copy-done.8, bf16[768,256]{1,0:T(8,128)(2,1)} %copy-done.9, bf16[768,256]{1,0:T(8,128)(2,1)} %collective-permute-done.14.refs_3_), custom_call_target="tpu_custom_call" | custom-call | flops 3000000 | bytes 3670016 | tf_op jit(solution)/shard_map/pallas_call | solution.py:81
  34.9 10.3 %all-to-all-start.1 = ((bf16[16,2,128,256]{3,2,1,0:T(8,128)(2,1)}), bf16[16,2,128,256]{3,2,1,0:T(8,128)(2,1)S(1)}, u32[]{:S(2)}, u32[]{:S(2)}) async-start(bf16[16,2,128,256]{3,2,1,0:T(8,128)(2,1)} %bitcast.42), calls=%async_computation.1 | async-start | bytes 4194304 | tf_op jit(solution)/shard_map/all_to_all | solution.py:345
  52.0 30.6 %collective-permute-done.4.refs_0_ = bf16[768,256]{1,0:T(8,128)(2,1)} collective-permute-done((bf16[768,256]{1,0:T(8,128)(2,1)}, bf16[768,256]{1,0:T(8,128)(2,1)}, u32[]{:S(2)}, u32[]{:S(2)}) %collective-permute-start.4) | collective-permute-done | bytes 393248 | tf_op jit(solution)/shard_map/ppermute | solution.py:43
  86.0 30.2 %collective-permute-done.8.refs_4_ = bf16[768,256]{1,0:T(8,128)(2,1)} collective-permute-done((bf16[768,256]{1,0:T(8,128)(2,1)}, bf16[768,256]{1,0:T(8,128)(2,1)}, u32[]{:S(2)}, u32[]{:S(2)}) %collective-permute-start.8) | collective-permute-done | bytes 393248 | tf_op jit(solution)/shard_map/ppermute | solution.py:43
  116.3 5.3 %shard_map.55 = bf16[32,128,512]{2,1,0:T(8,128)(2,1)} custom-call(s32[32]{0:T(128)} %get-tuple-element.14.chosen_ref, bf16[768,256]{1,0:T(8,128)(2,1)} %collective-permute-done.4.refs_0_, bf16[768,256]{1,0:T(8,128)(2,1)} %collective-permute-done.5.refs_1_, bf16[768,256]{1,0:T(8,128)(2,1)} %collective-permute-done.6.refs_2_, ...), custom_call_target="tpu_custom_call" | custom-call | flops 3000000 | bytes 7340032 | tf_op jit(solution)/shard_map/pallas_call | solution.py:81
  122.9 7.9 %all-to-all-start = ((bf16[16,2,128,512]{3,2,1,0:T(8,128)(2,1)}), bf16[16,2,128,512]{3,2,1,0:T(8,128)(2,1)}, u32[]{:S(2)}, u32[]{:S(2)}) async-start(bf16[16,2,128,512]{3,2,1,0:T(8,128)(2,1)} %bitcast.39), calls=%async_computation | async-start | bytes 8388608 | tf_op jit(solution)/shard_map/all_to_all | solution.py:345
  132.9 4.1 %collective-permute-start.22 = (bf16[768,256]{1,0:T(8,128)(2,1)S(1)}, bf16[768,256]{1,0:T(8,128)(2,1)S(1)}, u32[]{:S(2)}, u32[]{:S(2)}) collective-permute-start(bf16[768,256]{1,0:T(8,128)(2,1)S(1)} %get-tuple-element.17), channel_id=1, source_target_pairs={{0,13},{1,14},{2,15},{3,12},{4,1},{5,2},{6,3},{7,0},{8,5},{9,6},{1... | collective-permute-start | bytes 1179656 | tf_op jit(solution)/shard_map/ppermute | solution.py:43
  137.1 30.9 %collective-permute-done.19.refs_0_ = bf16[768,256]{1,0:T(8,128)(2,1)S(1)} collective-permute-done((bf16[768,256]{1,0:T(8,128)(2,1)}, bf16[768,256]{1,0:T(8,128)(2,1)S(1)}, u32[]{:S(2)}, u32[]{:S(2)}) %collective-permute-start.19) | collective-permute-done | bytes 393248 | tf_op jit(solution)/shard_map/ppermute | solution.py:43
  169.8 4.0 %shard_map.57 = bf16[32,128,256]{2,1,0:T(8,128)(2,1)} custom-call(s32[32]{0:T(128)} %get-tuple-element.14.chosen_ref, bf16[768,256]{1,0:T(8,128)(2,1)} %copy-done.10, bf16[768,256]{1,0:T(8,128)(2,1)} %copy-done.11, bf16[768,256]{1,0:T(8,128)(2,1)} %copy-done.12, bf16[768,256]{1,0:T(8,128)(2,1)} %copy-done.13), custom_call_target="tpu_custom_call" | custom-call | flops 3000000 | bytes 3670016 | tf_op jit(solution)/shard_map/pallas_call | solution.py:81
  173.8 50.5 %all-to-all-done = bf16[16,2,128,512]{3,2,1,0:T(8,128)(2,1)} async-done(((bf16[16,2,128,512]{3,2,1,0:T(8,128)(2,1)}), bf16[16,2,128,512]{3,2,1,0:T(8,128)(2,1)}, u32[]{:S(2)}, u32[]{:S(2)}) %all-to-all-start) | async-done | bytes 4194336 | tf_op jit(solution)/shard_map/all_to_all | solution.py:345
  224.3 5.5 %all-to-all-start.2 = ((bf16[16,2,128,256]{3,2,1,0:T(8,128)(2,1)}), bf16[16,2,128,256]{3,2,1,0:T(8,128)(2,1)}, u32[]{:S(2)}, u32[]{:S(2)}) async-start(bf16[16,2,128,256]{3,2,1,0:T(8,128)(2,1)} %bitcast.41), calls=%async_computation.2 | async-start | bytes 4194304 | tf_op jit(solution)/shard_map/all_to_all | solution.py:345
  234.0 3.7 %pack_keys.1 = bf16[3072,256]{1,0:T(8,128)(2,1)} custom-call(s32[24]{0:T(128)} %get-tuple-element.44.slot_ref, s32[24]{0:T(128)} %get-tuple-element.43.offset_ref, bf16[32,128,256]{2,1,0:T(8,128)(2,1)} %bitcast.40, f32[1024,128]{1,0:T(8,128)} %get-tuple-element.38.cos_ref, f32[1024,128]{1,0:T(8,128)} %get-tuple-element.37.sin_ref), custom_call_target="tpu_custom_call" | custom-call | flops 10000000 | bytes 5000000 | tf_op jit(solution)/shard_map/pack_keys/pallas_call | solution.py:113
  238.8 36.1 %collective-permute-done.15.k_ref = bf16[3072,256]{1,0:T(8,128)(2,1)S(1)} collective-permute-done((bf16[3072,256]{1,0:T(8,128)(2,1)}, bf16[3072,256]{1,0:T(8,128)(2,1)S(1)}, u32[]{:S(2)}, u32[]{:S(2)}) %collective-permute-start.15) | collective-permute-done | bytes 1572896 | tf_op jit(solution)/shard_map/ppermute | solution.py:35
  276.1 6.4 %attend.8 = bf16[768,256]{1,0:T(8,128)(2,1)} custom-call(s32[4,24]{1,0:T(4,128)} %pad_add_fusion.3.table_ref, s32[1]{0:T(128)} %bitcast.21.shard_ref, bf16[32,128,512]{2,1,0:T(8,128)(2,1)} %bitcast.24.q_ref.v_ref, bf16[3072,256]{1,0:T(8,128)(2,1)} %copy-done, bf16[32,128,512]{2,1,0:T(8,128)(2,1)} %bitcast.24.q_ref.v_ref, ...), custom_call_target="tpu_custom_call" | custom-call | flops 402653184 | bytes 4000000 | tf_op jit(solution)/shard_map/attend/pallas_call | solution.py:223
  284.0 6.3 %attend.9 = bf16[768,256]{1,0:T(8,128)(2,1)} custom-call(s32[4,24]{1,0:T(4,128)} %pad_add_fusion.3.table_ref, s32[1]{0:T(128)} %bitcast.27.shard_ref, bf16[32,128,512]{2,1,0:T(8,128)(2,1)} %bitcast.24.q_ref.v_ref, bf16[3072,256]{1,0:T(8,128)(2,1)} %copy-done, bf16[32,128,512]{2,1,0:T(8,128)(2,1)} %bitcast.24.q_ref.v_ref, ...), custom_call_target="tpu_custom_call" | custom-call | flops 402653184 | bytes 4000000 | tf_op jit(solution)/shard_map/attend/pallas_call | solution.py:223
  290.4 6.3 %attend.10 = bf16[768,256]{1,0:T(8,128)(2,1)} custom-call(s32[4,24]{1,0:T(4,128)} %pad_add_fusion.3.table_ref, s32[1]{0:T(128)} %bitcast.28.shard_ref, bf16[32,128,512]{2,1,0:T(8,128)(2,1)} %bitcast.24.q_ref.v_ref, bf16[3072,256]{1,0:T(8,128)(2,1)} %copy-done, bf16[32,128,512]{2,1,0:T(8,128)(2,1)} %bitcast.24.q_ref.v_ref, ...), custom_call_target="tpu_custom_call" | custom-call | flops 402653184 | bytes 4000000 | tf_op jit(solution)/shard_map/attend/pallas_call | solution.py:223
  299.7 6.4 %attend.12 = bf16[768,256]{1,0:T(8,128)(2,1)} custom-call(s32[4,24]{1,0:T(4,128)} %pad_add_fusion.3.table_ref, s32[1]{0:T(128)} %bitcast.21.shard_ref, bf16[32,128,256]{2,1,0:T(8,128)(2,1)} %bitcast.31.q_ref, bf16[3072,256]{1,0:T(8,128)(2,1)} %copy-done, bf16[32,128,512]{2,1,0:T(8,128)(2,1)} %bitcast.24.q_ref.v_ref, f32[1024,128]{1,0:T(8,128)} %get-tuple-element.38.cos_ref, ...), custom_call_target="tpu_custom_call" | custom-call | flops 402653184 | bytes 4000000 | tf_op jit(solution)/shard_map/attend/pallas_call | solution.py:223
  306.2 6.3 %attend.13 = bf16[768,256]{1,0:T(8,128)(2,1)} custom-call(s32[4,24]{1,0:T(4,128)} %pad_add_fusion.3.table_ref, s32[1]{0:T(128)} %bitcast.27.shard_ref, bf16[32,128,256]{2,1,0:T(8,128)(2,1)} %bitcast.31.q_ref, bf16[3072,256]{1,0:T(8,128)(2,1)} %copy-done, bf16[32,128,512]{2,1,0:T(8,128)(2,1)} %bitcast.24.q_ref.v_ref, f32[1024,128]{1,0:T(8,128)} %get-tuple-element.38.cos_ref, ...), custom_call_target="tpu_custom_call" | custom-call | flops 402653184 | bytes 4000000 | tf_op jit(solution)/shard_map/attend/pallas_call | solution.py:223
  313.2 6.3 %attend.14 = bf16[768,256]{1,0:T(8,128)(2,1)} custom-call(s32[4,24]{1,0:T(4,128)} %pad_add_fusion.3.table_ref, s32[1]{0:T(128)} %bitcast.28.shard_ref, bf16[32,128,256]{2,1,0:T(8,128)(2,1)} %bitcast.31.q_ref, bf16[3072,256]{1,0:T(8,128)(2,1)} %copy-done, bf16[32,128,512]{2,1,0:T(8,128)(2,1)} %bitcast.24.q_ref.v_ref, f32[1024,128]{1,0:T(8,128)} %get-tuple-element.38.cos_ref, ...), custom_call_target="tpu_custom_call" | custom-call | flops 402653184 | bytes 4000000 | tf_op jit(solution)/shard_map/attend/pallas_call | solution.py:223
  322.3 6.2 %attend.11.refs_3_ = bf16[768,256]{1,0:T(8,128)(2,1)} custom-call(s32[4,24]{1,0:T(4,128)} %pad_add_fusion.3.table_ref, s32[1]{0:T(128)} %bitcast.29.shard_ref, bf16[32,128,512]{2,1,0:T(8,128)(2,1)} %bitcast.24.q_ref.v_ref, bf16[3072,256]{1,0:T(8,128)(2,1)} %copy-done, bf16[32,128,512]{2,1,0:T(8,128)(2,1)} %bitcast.24.q_ref.v_ref, ...), custom_call_target="tpu_custom_call" | custom-call | flops 402653184 | bytes 4000000 | tf_op jit(solution)/shard_map/attend/pallas_call | solution.py:223
  328.6 6.2 %attend.15.refs_7_ = bf16[768,256]{1,0:T(8,128)(2,1)} custom-call(s32[4,24]{1,0:T(4,128)} %pad_add_fusion.3.table_ref, s32[1]{0:T(128)} %bitcast.29.shard_ref, bf16[32,128,256]{2,1,0:T(8,128)(2,1)} %bitcast.31.q_ref, bf16[3072,256]{1,0:T(8,128)(2,1)} %copy-done, bf16[32,128,512]{2,1,0:T(8,128)(2,1)} %bitcast.24.q_ref.v_ref, ...), custom_call_target="tpu_custom_call" | custom-call | flops 402653184 | bytes 4000000 | tf_op jit(solution)/shard_map/attend/pallas_call | solution.py:223
  (114 shorter events, 48.0 us)
Async XLA Ops:
  7.7 22.4 %collective-permute-start.12 = (bf16[768,256]{1,0:T(8,128)(2,1)S(1)}, bf16[768,256]{1,0:T(8,128)(2,1)S(1)}, u32[]{:S(2)}, u32[]{:S(2)}) collective-permute-start(bf16[768,256]{1,0:T(8,128)(2,1)S(1)} %get-tuple-element.23), channel_id=1, source_target_pairs={{0,4},{4,8},{8,12},{12,0},{1,5},{5,9},{9,13},{13,1},{2,6},{6,10},{... | collective-permute-start | bytes 1179656 | tf_op jit(solution)/shard_map/ppermute | solution.py:30
  8.9 21.1 %collective-permute-start.13 = (bf16[768,256]{1,0:T(8,128)(2,1)S(1)}, bf16[768,256]{1,0:T(8,128)(2,1)S(1)}, u32[]{:S(2)}, u32[]{:S(2)}) collective-permute-start(bf16[768,256]{1,0:T(8,128)(2,1)S(1)} %get-tuple-element.22), channel_id=1, source_target_pairs={{0,8},{4,12},{8,0},{12,4},{1,9},{5,13},{9,1},{13,5},{2,10},{6,14},... | collective-permute-start | bytes 1179656 | tf_op jit(solution)/shard_map/ppermute | solution.py:30
  12.7 15.5 %collective-permute-start.2 = (s32[2,4,6]{2,1,0:T(4,128)S(1)}, s32[2,4,6]{2,1,0:T(4,128)S(1)}, u32[]{:S(2)}, u32[]{:S(2)}) collective-permute-start(s32[2,4,6]{2,1,0:T(4,128)S(1)} %get-tuple-element.34), channel_id=1, source_target_pairs={{0,8},{4,12},{8,0},{12,4},{1,9},{5,13},{9,1},{13,5},{2,10},{6,14},... | collective-permute-start | bytes 584 | tf_op jit(solution)/shard_map/ppermute | solution.py:30
  34.9 86.6 %all-to-all-start.1 = ((bf16[16,2,128,256]{3,2,1,0:T(8,128)(2,1)}), bf16[16,2,128,256]{3,2,1,0:T(8,128)(2,1)S(1)}, u32[]{:S(2)}, u32[]{:S(2)}) async-start(bf16[16,2,128,256]{3,2,1,0:T(8,128)(2,1)} %bitcast.42), calls=%async_computation.1 | async-start | bytes 4194304 | tf_op jit(solution)/shard_map/all_to_all | solution.py:345
  45.3 37.3 %collective-permute-start.4 = (bf16[768,256]{1,0:T(8,128)(2,1)}, bf16[768,256]{1,0:T(8,128)(2,1)}, u32[]{:S(2)}, u32[]{:S(2)}) collective-permute-start(bf16[768,256]{1,0:T(8,128)(2,1)} %get-tuple-element.32), channel_id=1, source_target_pairs={{0,1},{1,2},{2,3},{3,0},{4,5},{5,6},{6,7},{7,4},{8,9},{9,10},{10,1... | collective-permute-start | bytes 1179656 | tf_op jit(solution)/shard_map/ppermute | solution.py:43
  46.6 36.0 %collective-permute-start.5 = (bf16[768,256]{1,0:T(8,128)(2,1)}, bf16[768,256]{1,0:T(8,128)(2,1)}, u32[]{:S(2)}, u32[]{:S(2)}) collective-permute-start(bf16[768,256]{1,0:T(8,128)(2,1)} %get-tuple-element.31), channel_id=1, source_target_pairs={{0,5},{1,6},{2,7},{3,4},{4,9},{5,10},{6,11},{7,8},{8,13},{9,14},{1... | collective-permute-start | bytes 1179656 | tf_op jit(solution)/shard_map/ppermute | solution.py:43
  46.6 38.0 %collective-permute-start.6 = (bf16[768,256]{1,0:T(8,128)(2,1)}, bf16[768,256]{1,0:T(8,128)(2,1)}, u32[]{:S(2)}, u32[]{:S(2)}) collective-permute-start(bf16[768,256]{1,0:T(8,128)(2,1)} %get-tuple-element.30), channel_id=1, source_target_pairs={{0,9},{1,10},{2,11},{3,8},{4,13},{5,14},{6,15},{7,12},{8,1},{9,2},... | collective-permute-start | bytes 1179656 | tf_op jit(solution)/shard_map/ppermute | solution.py:43
  48.7 37.4 %collective-permute-start.7 = (bf16[768,256]{1,0:T(8,128)(2,1)}, bf16[768,256]{1,0:T(8,128)(2,1)}, u32[]{:S(2)}, u32[]{:S(2)}) collective-permute-start(bf16[768,256]{1,0:T(8,128)(2,1)} %get-tuple-element.29), channel_id=1, source_target_pairs={{0,13},{1,14},{2,15},{3,12},{4,1},{5,2},{6,3},{7,0},{8,5},{9,6},{1... | collective-permute-start | bytes 1179656 | tf_op jit(solution)/shard_map/ppermute | solution.py:43
  50.7 65.6 %collective-permute-start.8 = (bf16[768,256]{1,0:T(8,128)(2,1)}, bf16[768,256]{1,0:T(8,128)(2,1)}, u32[]{:S(2)}, u32[]{:S(2)}) collective-permute-start(bf16[768,256]{1,0:T(8,128)(2,1)} %get-tuple-element.28), channel_id=1, source_target_pairs={{0,1},{1,2},{2,3},{3,0},{4,5},{5,6},{6,7},{7,4},{8,9},{9,10},{10,1... | collective-permute-start | bytes 1179656 | tf_op jit(solution)/shard_map/ppermute | solution.py:43
  82.6 33.7 %collective-permute-start.9 = (bf16[768,256]{1,0:T(8,128)(2,1)}, bf16[768,256]{1,0:T(8,128)(2,1)}, u32[]{:S(2)}, u32[]{:S(2)}) collective-permute-start(bf16[768,256]{1,0:T(8,128)(2,1)} %get-tuple-element.27), channel_id=1, source_target_pairs={{0,5},{1,6},{2,7},{3,4},{4,9},{5,10},{6,11},{7,8},{8,13},{9,14},{1... | collective-permute-start | bytes 1179656 | tf_op jit(solution)/shard_map/ppermute | solution.py:43
  82.6 33.7 %collective-permute-start.10 = (bf16[768,256]{1,0:T(8,128)(2,1)}, bf16[768,256]{1,0:T(8,128)(2,1)}, u32[]{:S(2)}, u32[]{:S(2)}) collective-permute-start(bf16[768,256]{1,0:T(8,128)(2,1)} %get-tuple-element.26), channel_id=1, source_target_pairs={{0,9},{1,10},{2,11},{3,8},{4,13},{5,14},{6,15},{7,12},{8,1},{9,2},... | collective-permute-start | bytes 1179656 | tf_op jit(solution)/shard_map/ppermute | solution.py:43
  84.6 31.7 %collective-permute-start.11 = (bf16[768,256]{1,0:T(8,128)(2,1)}, bf16[768,256]{1,0:T(8,128)(2,1)}, u32[]{:S(2)}, u32[]{:S(2)}) collective-permute-start(bf16[768,256]{1,0:T(8,128)(2,1)} %get-tuple-element.25), channel_id=1, source_target_pairs={{0,13},{1,14},{2,15},{3,12},{4,1},{5,2},{6,3},{7,0},{8,5},{9,6},{1... | collective-permute-start | bytes 1179656 | tf_op jit(solution)/shard_map/ppermute | solution.py:43
  122.9 101.4 %all-to-all-start = ((bf16[16,2,128,512]{3,2,1,0:T(8,128)(2,1)}), bf16[16,2,128,512]{3,2,1,0:T(8,128)(2,1)}, u32[]{:S(2)}, u32[]{:S(2)}) async-start(bf16[16,2,128,512]{3,2,1,0:T(8,128)(2,1)} %bitcast.39), calls=%async_computation | async-start | bytes 8388608 | tf_op jit(solution)/shard_map/all_to_all | solution.py:345
  130.7 37.2 %collective-permute-start.19 = (bf16[768,256]{1,0:T(8,128)(2,1)}, bf16[768,256]{1,0:T(8,128)(2,1)S(1)}, u32[]{:S(2)}, u32[]{:S(2)}) collective-permute-start(bf16[768,256]{1,0:T(8,128)(2,1)} %get-tuple-element.20), channel_id=1, source_target_pairs={{0,1},{1,2},{2,3},{3,0},{4,5},{5,6},{6,7},{7,4},{8,9},{9,10},{10,1... | collective-permute-start | bytes 1179656 | tf_op jit(solution)/shard_map/ppermute | solution.py:43
  130.8 37.2 %collective-permute-start.20 = (bf16[768,256]{1,0:T(8,128)(2,1)S(1)}, bf16[768,256]{1,0:T(8,128)(2,1)S(1)}, u32[]{:S(2)}, u32[]{:S(2)}) collective-permute-start(bf16[768,256]{1,0:T(8,128)(2,1)S(1)} %get-tuple-element.19), channel_id=1, source_target_pairs={{0,5},{1,6},{2,7},{3,4},{4,9},{5,10},{6,11},{7,8},{8,13},{9,14},{1... | collective-permute-start | bytes 1179656 | tf_op jit(solution)/shard_map/ppermute | solution.py:43
  130.8 37.2 %collective-permute-start.21 = (bf16[768,256]{1,0:T(8,128)(2,1)S(1)}, bf16[768,256]{1,0:T(8,128)(2,1)S(1)}, u32[]{:S(2)}, u32[]{:S(2)}) collective-permute-start(bf16[768,256]{1,0:T(8,128)(2,1)S(1)} %get-tuple-element.18), channel_id=1, source_target_pairs={{0,9},{1,10},{2,11},{3,8},{4,13},{5,14},{6,15},{7,12},{8,1},{9,2},... | collective-permute-start | bytes 1179656 | tf_op jit(solution)/shard_map/ppermute | solution.py:43
  132.9 35.1 %collective-permute-start.22 = (bf16[768,256]{1,0:T(8,128)(2,1)S(1)}, bf16[768,256]{1,0:T(8,128)(2,1)S(1)}, u32[]{:S(2)}, u32[]{:S(2)}) collective-permute-start(bf16[768,256]{1,0:T(8,128)(2,1)S(1)} %get-tuple-element.17), channel_id=1, source_target_pairs={{0,13},{1,14},{2,15},{3,12},{4,1},{5,2},{6,3},{7,0},{8,5},{9,6},{1... | collective-permute-start | bytes 1179656 | tf_op jit(solution)/shard_map/ppermute | solution.py:43
  224.3 75.5 %all-to-all-start.2 = ((bf16[16,2,128,256]{3,2,1,0:T(8,128)(2,1)}), bf16[16,2,128,256]{3,2,1,0:T(8,128)(2,1)}, u32[]{:S(2)}, u32[]{:S(2)}) async-start(bf16[16,2,128,256]{3,2,1,0:T(8,128)(2,1)} %bitcast.41), calls=%async_computation.2 | async-start | bytes 4194304 | tf_op jit(solution)/shard_map/all_to_all | solution.py:345
  237.6 37.3 %collective-permute-start.15 = (bf16[3072,256]{1,0:T(8,128)(2,1)}, bf16[3072,256]{1,0:T(8,128)(2,1)S(1)}, u32[]{:S(2)}, u32[]{:S(2)}) collective-permute-start(bf16[3072,256]{1,0:T(8,128)(2,1)} %pack_keys.1), channel_id=1, source_target_pairs={{0,1},{1,2},{2,3},{3,0},{4,5},{5,6},{6,7},{7,4},{8,9},{9,10},{10,1... | collective-permute-start | bytes 4718600 | tf_op jit(solution)/shard_map/ppermute | solution.py:35
  282.5 37.0 %collective-permute-start.16 = (bf16[768,256]{1,0:T(8,128)(2,1)}, bf16[768,256]{1,0:T(8,128)(2,1)S(1)}, u32[]{:S(2)}, u32[]{:S(2)}) collective-permute-start(bf16[768,256]{1,0:T(8,128)(2,1)} %attend.8), channel_id=1, source_target_pairs={{0,8},{4,12},{8,0},{12,4},{1,9},{5,13},{9,1},{13,5},{2,10},{6,14},... | collective-permute-start | bytes 1179656 | tf_op jit(solution)/shard_map/ppermute | solution.py:30
  290.3 44.5 %collective-permute-start.17 = (bf16[768,256]{1,0:T(8,128)(2,1)}, bf16[768,256]{1,0:T(8,128)(2,1)S(1)}, u32[]{:S(2)}, u32[]{:S(2)}) collective-permute-start(bf16[768,256]{1,0:T(8,128)(2,1)} %attend.9), channel_id=1, source_target_pairs={{0,4},{4,8},{8,12},{12,0},{1,5},{5,9},{9,13},{13,1},{2,6},{6,10},{... | collective-permute-start | bytes 1179656 | tf_op jit(solution)/shard_map/ppermute | solution.py:30
  296.7 38.1 %collective-permute-start.18 = (bf16[768,256]{1,0:T(8,128)(2,1)}, bf16[768,256]{1,0:T(8,128)(2,1)S(1)}, u32[]{:S(2)}, u32[]{:S(2)}) collective-permute-start(bf16[768,256]{1,0:T(8,128)(2,1)} %attend.10), channel_id=1, source_target_pairs={{0,12},{4,0},{8,4},{12,8},{1,13},{5,1},{9,5},{13,9},{2,14},{6,2},{... | collective-permute-start | bytes 1179656 | tf_op jit(solution)/shard_map/ppermute | solution.py:30
  306.1 28.7 %collective-permute-start.23 = (bf16[768,256]{1,0:T(8,128)(2,1)}, bf16[768,256]{1,0:T(8,128)(2,1)S(1)}, u32[]{:S(2)}, u32[]{:S(2)}) collective-permute-start(bf16[768,256]{1,0:T(8,128)(2,1)} %attend.12), channel_id=1, source_target_pairs={{0,8},{4,12},{8,0},{12,4},{1,9},{5,13},{9,1},{13,5},{2,10},{6,14},... | collective-permute-start | bytes 1179656 | tf_op jit(solution)/shard_map/ppermute | solution.py:30
  312.5 22.3 %collective-permute-start.24 = (bf16[768,256]{1,0:T(8,128)(2,1)}, bf16[768,256]{1,0:T(8,128)(2,1)S(1)}, u32[]{:S(2)}, u32[]{:S(2)}) collective-permute-start(bf16[768,256]{1,0:T(8,128)(2,1)} %attend.13), channel_id=1, source_target_pairs={{0,4},{4,8},{8,12},{12,0},{1,5},{5,9},{9,13},{13,1},{2,6},{6,10},{... | collective-permute-start | bytes 1179656 | tf_op jit(solution)/shard_map/ppermute | solution.py:30
  (19 other events, 81.1 us)
